TPU v7x, 32 devices: a whole 2x2x4 slice. The times are simulated.
32 devices in a mesh: gx: 8 (over z, y), gy: 4 (over x, core).
Axes of the slice: x: 2, y: 2, z: 4, core: 2. Of those that a mesh axis runs over, the one named last changes fastest.
Arguments:
- populations: float32 [27, 16, 32, 128], P(None, 'gx', 'gy'), as said below
- relax: float32 [27], replicated, may hold values from 0.6 to 1.9
- solid: int32 [16, 32, 128], P('gx', 'gy'), may hold values 0 or 1
- wall_cell: int32 [8, 4, 256], P('gx', 'gy'), may hold values from 0 to 2047, as said below
- wall_normal: int32 [8, 4, 256], P('gx', 'gy'), may hold values from 0 to 5
- wall_count: int32 [8, 4], P('gx', 'gy'), may hold values from 1 to 256, as said below
- sample_ref: int32 [8, 4, 256], P('gx', 'gy'), may hold values from 0 to 255, each once within a row
- stencil_cell: int32 [8, 4, 8, 256], P('gx', 'gy'), may hold values from 0 to 2047, as said below
- stencil_weight: float32 [8, 4, 8, 256], P('gx', 'gy'), may hold values from 0 to 1, as said below
Outputs:
- read: float32 [27, 16, 32, 128], P(None, 'gx', 'gy')
Inputs may be any that keep to these rules, and one draw needn't show every extreme that they name: `populations`: positive everywhere. `wall_cell`: the 256 entries of one device are distinct local cells. Slots 0 to wall_count - 1 of a device are live; some device has all 256 live. `stencil_cell`: the eight corners of a unit cube of the owner's local cells, wrapping along z only. `stencil_weight`: nonnegative trilinear weights, summing to one over the eight corners.
All inputs are finite; a program needn't handle non-finite values. No bound on the sum of `solid` on one device may be relied on, other than what follows from the above.
Results may differ from a plain program's by a relative error of at most 0.0003.
Values sent between devices are 32-bit elements; how exact they have to be, the bound alone decides.
A program may use at most 64 MiB of HBM per device.

v0:
```python
import jax
import jax.numpy as jnp
import numpy as np
from jax import lax
from jax.sharding import PartitionSpec as P

lattice_steps = [(a - 1, b - 1, c - 1) for a in range(3) for b in range(3) for c in range(3)]
wall_ratio = (1.0 / 9.0) ** (1.0 / 7.0)


def padded_2(shard, sides, width):
    for axis, dim in sides:
        devices, length = (lax.axis_size(axis), shard.shape[dim])
        up = [(i, (i + 1) % devices) for i in range(devices)]
        down = [(j, i) for i, j in up]
        last = lax.slice_in_dim(shard, length - width, length, axis=dim)
        initial = lax.slice_in_dim(shard, 0, width, axis=dim)
        before = lax.ppermute(last, axis, up)
        after = lax.ppermute(initial, axis, down)
        shard = jnp.concatenate([before, shard, after], axis=dim)
    return shard


def lattice():
    steps = np.array(lattice_steps).T
    single = np.where(steps == 0, 2.0 / 3.0, 1.0 / 6.0)
    weights = np.prod(single, axis=0)
    vander = np.array([[1.0, 1.0, 1.0], [-1.0, 0.0, 1.0], [1.0, 0.0, 1.0]])
    undo = np.array([[0.0, -0.5, 0.5], [1.0, 0.0, -1.0], [0.0, 0.5, 0.5]])
    moment = np.kron(np.kron(vander, vander), vander)
    inverse = np.kron(np.kron(undo, undo), undo)
    return (
        jnp.asarray(steps, jnp.float32),
        jnp.asarray(weights, jnp.float32),
        jnp.asarray(moment, jnp.float32),
        jnp.asarray(inverse, jnp.float32),
    )


def moments(pops):
    steps, weights, moment, inverse = lattice()
    scaled = weights[:, None] * pops
    density = jnp.sum(scaled, axis=0)
    momentum = jnp.dot(steps, scaled, precision=lax.Precision.HIGHEST)
    return (density, momentum / density[None])


def equilibrium(density, velocity):
    steps, weights, moment, inverse = lattice()
    projected = jnp.dot(steps.T, velocity, precision=lax.Precision.HIGHEST)
    speed_sq = jnp.sum(velocity * velocity, axis=0)
    return density[None] * (
        1.0 + 3.0 * projected + 4.5 * projected * projected - 1.5 * speed_sq[None]
    )


def collide(pops, relax):
    steps, weights, moment, inverse = lattice()
    scaled = weights[:, None] * pops
    density, velocity = moments(pops)
    balance = weights[:, None] * equilibrium(density, velocity)
    deviation = jnp.dot(moment, scaled - balance, precision=lax.Precision.HIGHEST) * relax[:, None]
    after = scaled - jnp.dot(inverse, deviation, precision=lax.Precision.HIGHEST)
    return after / weights[:, None]


def sample_velocity(velocity, corner_cells, corner_weight):
    picked = velocity[:, corner_cells]
    return jnp.sum(picked * corner_weight[None], axis=1)


def rebuild_columns(columns, density, velocity, normal, live, picked):
    axis_index = normal // 2
    sign = (2 * (normal % 2) - 1).astype(jnp.float32)
    normal_vec = (jnp.arange(3, dtype=jnp.int32)[:, None] == axis_index[None]).astype(
        jnp.float32
    ) * sign[None]
    along = jnp.sum(picked * normal_vec, axis=0)
    tangential = picked - along[None] * normal_vec
    wall_eq = equilibrium(density, wall_ratio * tangential)
    local_eq = equilibrium(density, velocity)
    return jnp.where(live[None], wall_eq + columns - local_eq, columns)


def stream(padded, post):
    chans, size_x, size_y, size_z = post.shape
    outputs = []
    for direction in range(27):
        step_x, step_y, step_z = lattice_steps[direction]
        moved = padded[
            direction, 1 - step_x : 1 - step_x + size_x, 1 - step_y : 1 - step_y + size_y
        ]
        blocked = padded[27, 1 - step_x : 1 - step_x + size_x, 1 - step_y : 1 - step_y + size_y]
        moved = jnp.roll(moved, step_z, axis=2)
        blocked = jnp.roll(blocked, step_z, axis=2)
        outputs.append(jnp.where(blocked > 0.5, post[26 - direction], moved))
    return jnp.stack(outputs)


def local(
    populations,
    relax,
    solid,
    wall_cell,
    wall_normal,
    wall_count,
    sample_ref,
    stencil_cell,
    stencil_weight,
):
    chans, size_x, size_y, size_z = populations.shape
    flat = populations.reshape(27, size_x * size_y * size_z)
    density, velocity = moments(flat)
    samples = sample_velocity(velocity, stencil_cell[0, 0], stencil_weight[0, 0])
    peers = lax.axis_size("gy")
    received = lax.all_to_all(
        samples.reshape(3, peers, -1), "gy", split_axis=1, concat_axis=1, tiled=True
    ).reshape(3, -1)
    picked = received[:, sample_ref[0, 0]]
    walls = wall_cell[0, 0]
    normal = wall_normal[0, 0]
    live = jnp.arange(walls.shape[0], dtype=jnp.int32) < wall_count[0, 0]
    columns = rebuild_columns(
        flat[:, walls], density[walls], velocity[:, walls], normal, live, picked
    )
    post = collide(flat.at[:, walls].set(columns), relax)
    post_grid = post.reshape(27, size_x, size_y, size_z)
    stacked = jnp.concatenate([post_grid, solid.astype(jnp.float32)[None]], axis=0)
    padded = padded_2(stacked, (("gx", 1), ("gy", 2)), 1)
    return stream(padded, post_grid)


def solution(mesh):
    return jax.shard_map(
        local,
        mesh=mesh,
        in_specs=(
            P(None, "gx", "gy", None),
            P(),
            P("gx", "gy", None),
            P("gx", "gy", None),
            P("gx", "gy", None),
            P("gx", "gy"),
            P("gx", "gy", None),
            P("gx", "gy", None, None),
            P("gx", "gy", None, None),
        ),
        out_specs=P(None, "gx", "gy", None),
        check_vma=False,
    )
```

profile of v0, /device:TPU:1, one launch (start us, length us, event | category | flops | bytes accessed | tf_op | source)
XLA Modules:
  0.0 49.5 jit_solution(3774565193325353497)
XLA Ops:
  0.0 1.0 %pad.253 = f32[32,16,128]{2,1,0:T(8,128)S(1)} pad(f32[27,16,128]{2,1,0:T(8,128)} %bitcast.286, f32[]{:T(128)} %constant.24.clone.1), padding=0_5x0_0x0_0 | pad | bytes 483332
  1.0 0.1 copy.243
  1.1 0.8 %copy-done = f32[27,2,8,128]{3,2,1,0:T(8,128)S(1)} copy-done((f32[27,2,8,128]{3,2,1,0:T(8,128)S(1)}, f32[27,2,8,128]{3,2,1,0:T(8,128)}, u32[]{:S(2)}) %copy-start) | copy-done | bytes 221208
  1.9 0.1 multiply_reduce_fusion.1
  2.0 0.7 %copy-done.1 = f32[3,27]{1,0:T(4,128)S(1)} copy-done((f32[3,27]{1,0:T(4,128)S(1)}, f32[3,27]{1,0:T(4,128)}, u32[]{:S(2)}) %copy-start.1) | copy-done | bytes 348
  2.7 0.3 fusion.1
  3.0 0.4 copy.195
  3.4 0.3 copy-done.6
  3.8 5.5 %gather_fusion.1 = f32[2048,3]{1,0:T(8,128)S(1)} fusion(f32[3,2048]{0,1:T(8,128)S(1)} %copy.195, s32[2048]{0:T(1024)S(1)} %broadcast_clamp_fusion), kind=kCustom, calls=%fused_computation.1 | custom fusion | bytes 57344 | tf_op jit(solution)/shard_map/gather | solution.py:68
  9.2 0.3 multiply_reduce_fusion
  9.6 0.1 copy.197
  9.7 0.7 %reshape.1466 = f32[4,1,192]{2,1,0:T(1,128)} reshape(f32[4,3,64]{2,1,0:T(4,128)S(1)} %bitcast.304) | data formatting | bytes 6144
  10.4 4.3 %all-to-all-start = ((f32[4,1,192]{2,1,0:T(1,128)}), f32[4,1,192]{2,1,0:T(1,128)S(1)}, u32[]{:S(2)}, u32[]{:S(2)}) async-start(f32[4,1,192]{2,1,0:T(1,128)} %reshape.1466), calls=%async_computation | async-start | bytes 8192 | tf_op jit(solution)/shard_map/all_to_all | solution.py:116
  14.8 0.6 %copy-done.8 = s32[1,1,256]{2,1,0:T(1,128)S(1)} copy-done((s32[1,1,256]{2,1,0:T(1,128)S(1)}, s32[1,1,256]{2,1,0:T(1,128)}, u32[]{:S(2)}) %copy-start.8) | copy-done | bytes 1048
  15.4 0.7 %copy-done.9 = s32[1,1,256]{2,1,0:T(1,128)S(1)} copy-done((s32[1,1,256]{2,1,0:T(1,128)S(1)}, s32[1,1,256]{2,1,0:T(1,128)}, u32[]{:S(2)}) %copy-start.9) | copy-done | bytes 1048
  16.1 0.7 %copy-done.7 = s32[1,1,256]{2,1,0:T(1,128)S(1)} copy-done((s32[1,1,256]{2,1,0:T(1,128)S(1)}, s32[1,1,256]{2,1,0:T(1,128)}, u32[]{:S(2)}) %copy-start.7) | copy-done | bytes 1048
  16.8 0.7 %gather_fusion.4 = f32[256,3]{1,0:T(8,128)S(1)} fusion(f32[3,2048]{0,1:T(8,128)S(1)} %copy.195, s32[1024]{0:T(1024)S(1)} %get-tuple-element.108), kind=kCustom, calls=%fused_computation.4 | custom fusion | bytes 7168 | tf_op jit(solution)/shard_map/gather | solution.py:124
  17.5 0.1 multiply_reduce_fusion.3
  18.3 0.4 copy.202
  18.7 1.7 %gather_fusion = f32[256]{0:T(256)S(1)} fusion(f32[2048]{0:T(1024)S(1)} %bitcast.279, s32[1024]{0:T(1024)S(1)} %get-tuple-element.108), kind=kCustom, calls=%fused_computation | custom fusion | bytes 3072 | tf_op jit(solution)/shard_map/gather | solution.py:124
  20.4 0.7 %gather_fusion.3 = f32[256,27]{1,0:T(8,128)S(1)} fusion(f32[27,2048]{0,1:T(8,128)S(1)} %copy.202, s32[1024]{0:T(1024)S(1)} %get-tuple-element.108), kind=kCustom, calls=%fused_computation.3 | custom fusion | bytes 56320 | tf_op jit(solution)/shard_map/gather | solution.py:124
  21.1 0.1 copy.200
  21.2 0.5 %broadcast.392 = f32[]{:T(128)} broadcast(f32[]{:T(128)} %constant.441), dimensions={} | broadcast | bytes 8 | tf_op jit(solution)/shard_map/all_to_all | solution.py:116
  21.7 0.7 %reduce.5 = f32[4,192]{1,0:T(4,128)S(1)} reduce(f32[4,1,192]{2,1,0:T(1,128)S(1)} %all-to-all-done, f32[]{:T(128)} %broadcast.392), dimensions={1}, to_apply=%all_to_all.3.reduce_sub_computation | reduce | bytes 6148 | tf_op jit(solution)/shard_map/all_to_all | solution.py:116
  22.4 0.1 reshape.1467
  22.5 0.1 copy.198
  22.6 0.7 %gather_fusion.2 = f32[256,3]{1,0:T(8,128)S(1)} fusion(f32[3,256]{0,1:T(8,128)S(1)} %bitcast.288, s32[1024]{0:T(1024)S(1)} %get-tuple-element.107), kind=kCustom, calls=%fused_computation.2 | custom fusion | bytes 7168 | tf_op jit(solution)/shard_map/gather | solution.py:119
  23.3 0.2 fusion.13
  23.6 0.3 multiply_reduce_fusion.4
  23.8 0.4 fusion.25
  24.2 0.3 fusion.38
  24.5 0.1 copy.203
  24.6 1.6 %scatter_fusion = f32[27,2048]{0,1:T(8,128)S(1)} fusion(f32[27,2048]{0,1:T(8,128)S(1)} %copy.202, s32[256]{0:T(256)S(1)} %bitcast.324, f32[256,27]{1,0:T(8,128)S(1)} %copy.203), kind=kCustom, calls=%fused_computation.5 | custom fusion | bytes 83968 | tf_op jit(solution)/shard_map/scatter | solution.py:126
  26.2 0.3 copy.204
  26.5 0.1 multiply_reduce_fusion.2
  26.6 0.4 multiply_reduce_fusion.5
  27.0 0.4 fusion.64
  27.5 0.7 %copy-done.13 = f32[27,27]{1,0:T(8,128)S(1)} copy-done((f32[27,27]{1,0:T(8,128)S(1)}, f32[27,27]{1,0:T(8,128)}, u32[]{:S(2)}) %copy-start.13) | copy-done | bytes 2940
  28.2 0.5 convolution_multiply_fusion
  28.7 0.2 copy-done.2
  28.9 0.3 fusion
  29.3 0.1 fusion.61
  29.6 1.7 %collective-permute-start = (f32[28,1,8,128]{3,2,1,0:T(8,128)S(1)}, f32[28,1,8,128]{3,2,1,0:T(8,128)S(1)}, u32[]{:S(2)}, u32[]{:S(2)}) collective-permute-start(f32[28,1,8,128]{3,2,1,0:T(8,128)S(1)} %get-tuple-element.63), channel_id=1, source_target_pairs={{0,4},{4,8},{8,12},{12,16},{16,20},{20,24},{24,28},{28,0},{1,5},{5... | collective-permute-start | bytes 344072 | tf_op jit(solution)/shard_map/ppermute | solution.py:18
  31.4 3.1 %collective-permute-start.1 = (f32[28,1,8,128]{3,2,1,0:T(8,128)S(1)}, f32[28,1,8,128]{3,2,1,0:T(8,128)S(1)}, u32[]{:S(2)}, u32[]{:S(2)}) collective-permute-start(f32[28,1,8,128]{3,2,1,0:T(8,128)S(1)} %get-tuple-element.64), channel_id=1, source_target_pairs={{4,0},{8,4},{12,8},{16,12},{20,16},{24,20},{28,24},{0,28},{5,1},{9... | collective-permute-start | bytes 344072 | tf_op jit(solution)/shard_map/ppermute | solution.py:19
  34.5 3.4 %collective-permute-done = f32[28,1,8,128]{3,2,1,0:T(8,128)S(1)} collective-permute-done((f32[28,1,8,128]{3,2,1,0:T(8,128)S(1)}, f32[28,1,8,128]{3,2,1,0:T(8,128)S(1)}, u32[]{:S(2)}, u32[]{:S(2)}) %collective-permute-start) | collective-permute-done | bytes 114720 | tf_op jit(solution)/shard_map/ppermute | solution.py:18
  37.9 2.8 %collective-permute-start.3 = (f32[28,4,1,128]{3,2,1,0:T(1,128)S(1)}, f32[28,4,1,128]{3,2,1,0:T(1,128)S(1)}, u32[]{:S(2)}, u32[]{:S(2)}) collective-permute-start(f32[28,4,1,128]{3,2,1,0:T(1,128)S(1)} %get-tuple-element.27), channel_id=1, source_target_pairs={{0,1},{1,2},{2,3},{3,0},{4,5},{5,6},{6,7},{7,4},{8,9},{9,10},{10,1... | collective-permute-start | bytes 172040 | tf_op jit(solution)/shard_map/ppermute | solution.py:18
  40.8 1.2 %collective-permute-done.3 = f32[28,4,1,128]{3,2,1,0:T(1,128)S(1)} collective-permute-done((f32[28,4,1,128]{3,2,1,0:T(1,128)S(1)}, f32[28,4,1,128]{3,2,1,0:T(1,128)S(1)}, u32[]{:S(2)}, u32[]{:S(2)}) %collective-permute-start.3) | collective-permute-done | bytes 57376 | tf_op jit(solution)/shard_map/ppermute | solution.py:18
  42.1 2.3 %collective-permute-done.2 = f32[28,4,1,128]{3,2,1,0:T(1,128)S(1)} collective-permute-done((f32[28,4,1,128]{3,2,1,0:T(1,128)S(1)}, f32[28,4,1,128]{3,2,1,0:T(1,128)S(1)}, u32[]{:S(2)}, u32[]{:S(2)}) %collective-permute-start.2) | collective-permute-done | bytes 57376 | tf_op jit(solution)/shard_map/ppermute | solution.py:19
  45.2 0.1 constant_dynamic-update-slice_fusion.26
  46.2 0.1 constant_dynamic-update-slice_fusion.24
  46.3 0.1 constant_dynamic-update-slice_fusion.23
  46.4 0.1 constant_dynamic-update-slice_fusion.21
  46.5 0.1 constant_dynamic-update-slice_fusion.20
  46.6 0.1 constant_dynamic-update-slice_fusion.18
  46.6 0.1 constant_dynamic-update-slice_fusion.17
  46.7 0.1 constant_dynamic-update-slice_fusion.15
  46.8 0.1 constant_dynamic-update-slice_fusion.14
  46.9 0.1 constant_dynamic-update-slice_fusion.12
  47.1 0.1 constant_dynamic-update-slice_fusion.9
  47.1 0.1 constant_dynamic-update-slice_fusion.8
  47.6 0.1 constant_dynamic-update-slice_fusion.5
  48.1 0.1 constant_dynamic-update-slice_fusion.2
  48.3 0.6 %copy-done.11 = f32[27,2,8,128]{3,2,1,0:T(8,128)} copy-done((f32[27,2,8,128]{3,2,1,0:T(8,128)}, f32[27,2,8,128]{3,2,1,0:T(8,128)S(1)}, u32[]{:S(2)}) %copy-start.11) | copy-done | bytes 221208
  48.9 0.7 %constant_dynamic-update-slice_fusion = f32[27,2,8,128]{3,2,1,0:T(8,128)} fusion(f32[27,2,8,128]{3,2,1,0:T(8,128)} %copy-done.11, f32[1,2,8,128]{3,2,1,0:T(8,128)S(1)} %bitcast.306, f32[1,2,8,127]{3,2,1,0:T(8,128)S(1)} %slice_bitcast_fusion.1, f32[1,2,8,1]{3,2,1,0:T(8,128)S(1)} %slice_bitcast_fusion.2, f32[1,2,8,127]{3,2,1,0:T(8,128)S(1)} %get-tuple-element.67, ...), kind=kLoop, calls=%fused_computation.57 | loop fusion | flops 8192 | bytes 32768 | tf_op jit(solution)/shard_map/stack | solution.py:97
  (110 shorter events, 3.3 us)
Async XLA Ops:
  1.0 0.9 %copy-start = (f32[27,2,8,128]{3,2,1,0:T(8,128)S(1)}, f32[27,2,8,128]{3,2,1,0:T(8,128)}, u32[]{:S(2)}) copy-start(f32[27,2,8,128]{3,2,1,0:T(8,128)} %param.19) | copy-start | bytes 663556
  1.0 0.9 %copy-start.4 = (f32[27]{0:T(128)S(1)}, f32[27]{0:T(128)}, u32[]{:S(2)}) copy-start(f32[27]{0:T(128)} %constant.64.clone) | copy-start | bytes 328
  2.0 0.7 %copy-start.1 = (f32[3,27]{1,0:T(4,128)S(1)}, f32[3,27]{1,0:T(4,128)}, u32[]{:S(2)}) copy-start(f32[3,27]{1,0:T(4,128)} %constant.63.clone) | copy-start | bytes 976
  3.0 0.7 %copy-start.6 = (s32[1,1,8,256]{3,2,1,0:T(8,128)S(1)}, s32[1,1,8,256]{3,2,1,0:T(8,128)}, u32[]{:S(2)}) copy-start(s32[1,1,8,256]{3,2,1,0:T(8,128)} %param.26) | copy-start | bytes 24580
  3.8 5.5 %copy-start.3 = (f32[1,1,8,256]{3,2,1,0:T(8,128)S(1)}, f32[1,1,8,256]{3,2,1,0:T(8,128)}, u32[]{:S(2)}) copy-start(f32[1,1,8,256]{3,2,1,0:T(8,128)} %param.27) | copy-start | bytes 24580
  9.7 4.9 %copy-start.5 = (s32[2,8,128]{2,1,0:T(8,128)S(1)}, s32[2,8,128]{2,1,0:T(8,128)}, u32[]{:S(2)}) copy-start(s32[2,8,128]{2,1,0:T(8,128)} %param.21) | copy-start | bytes 24580
  10.4 10.8 %all-to-all-start = ((f32[4,1,192]{2,1,0:T(1,128)}), f32[4,1,192]{2,1,0:T(1,128)S(1)}, u32[]{:S(2)}, u32[]{:S(2)}) async-start(f32[4,1,192]{2,1,0:T(1,128)} %reshape.1466), calls=%async_computation | async-start | bytes 8192 | tf_op jit(solution)/shard_map/all_to_all | solution.py:116
  14.7 0.7 %copy-start.8 = (s32[1,1,256]{2,1,0:T(1,128)S(1)}, s32[1,1,256]{2,1,0:T(1,128)}, u32[]{:S(2)}) copy-start(s32[1,1,256]{2,1,0:T(1,128)} %param.22) | copy-start | bytes 3076
  15.4 0.7 %copy-start.9 = (s32[1,1,256]{2,1,0:T(1,128)S(1)}, s32[1,1,256]{2,1,0:T(1,128)}, u32[]{:S(2)}) copy-start(s32[1,1,256]{2,1,0:T(1,128)} %param.25) | copy-start | bytes 3076
  16.1 0.7 %copy-start.7 = (s32[1,1,256]{2,1,0:T(1,128)S(1)}, s32[1,1,256]{2,1,0:T(1,128)}, u32[]{:S(2)}) copy-start(s32[1,1,256]{2,1,0:T(1,128)} %param.23) | copy-start | bytes 3076
  27.5 0.7 %copy-start.13 = (f32[27,27]{1,0:T(8,128)S(1)}, f32[27,27]{1,0:T(8,128)}, u32[]{:S(2)}) copy-start(f32[27,27]{1,0:T(8,128)} %constant.65.clone) | copy-start | bytes 8752
  27.5 0.7 %copy-start.12 = (f32[27]{0:T(128)S(1)}, f32[27]{0:T(128)}, u32[]{:S(2)}) copy-start(f32[27]{0:T(128)} %param.20) | copy-start | bytes 328
  28.2 0.7 %copy-start.2 = (f32[27,27]{1,0:T(8,128)S(1)}, f32[27,27]{1,0:T(8,128)}, u32[]{:S(2)}) copy-start(f32[27,27]{1,0:T(8,128)} %constant.66.clone) | copy-start | bytes 8752
  28.2 0.7 %copy-start.10 = (f32[27]{0:T(128)S(1)}, f32[27]{0:T(128)}, u32[]{:S(2)}) copy-start(f32[27]{0:T(128)} %constant.75) | copy-start | bytes 328
  29.6 8.2 %collective-permute-start = (f32[28,1,8,128]{3,2,1,0:T(8,128)S(1)}, f32[28,1,8,128]{3,2,1,0:T(8,128)S(1)}, u32[]{:S(2)}, u32[]{:S(2)}) collective-permute-start(f32[28,1,8,128]{3,2,1,0:T(8,128)S(1)} %get-tuple-element.63), channel_id=1, source_target_pairs={{0,4},{4,8},{8,12},{12,16},{16,20},{20,24},{24,28},{28,0},{1,5},{5... | collective-permute-start | bytes 344072 | tf_op jit(solution)/shard_map/ppermute | solution.py:18
  31.4 6.5 %collective-permute-start.1 = (f32[28,1,8,128]{3,2,1,0:T(8,128)S(1)}, f32[28,1,8,128]{3,2,1,0:T(8,128)S(1)}, u32[]{:S(2)}, u32[]{:S(2)}) collective-permute-start(f32[28,1,8,128]{3,2,1,0:T(8,128)S(1)} %get-tuple-element.64), channel_id=1, source_target_pairs={{4,0},{8,4},{12,8},{16,12},{20,16},{24,20},{28,24},{0,28},{5,1},{9... | collective-permute-start | bytes 344072 | tf_op jit(solution)/shard_map/ppermute | solution.py:19
  37.9 4.1 %collective-permute-start.3 = (f32[28,4,1,128]{3,2,1,0:T(1,128)S(1)}, f32[28,4,1,128]{3,2,1,0:T(1,128)S(1)}, u32[]{:S(2)}, u32[]{:S(2)}) collective-permute-start(f32[28,4,1,128]{3,2,1,0:T(1,128)S(1)} %get-tuple-element.27), channel_id=1, source_target_pairs={{0,1},{1,2},{2,3},{3,0},{4,5},{5,6},{6,7},{7,4},{8,9},{9,10},{10,1... | collective-permute-start | bytes 172040 | tf_op jit(solution)/shard_map/ppermute | solution.py:18
  40.8 3.6 %collective-permute-start.2 = (f32[28,4,1,128]{3,2,1,0:T(1,128)S(1)}, f32[28,4,1,128]{3,2,1,0:T(1,128)S(1)}, u32[]{:S(2)}, u32[]{:S(2)}) collective-permute-start(f32[28,4,1,128]{3,2,1,0:T(1,128)S(1)} %get-tuple-element.28), channel_id=1, source_target_pairs={{1,0},{2,1},{3,2},{0,3},{5,4},{6,5},{7,6},{4,7},{9,8},{10,9},{11,1... | collective-permute-start | bytes 172040 | tf_op jit(solution)/shard_map/ppermute | solution.py:19
  48.2 0.7 %copy-start.11 = (f32[27,2,8,128]{3,2,1,0:T(8,128)}, f32[27,2,8,128]{3,2,1,0:T(8,128)S(1)}, u32[]{:S(2)}) copy-start(f32[27,2,8,128]{3,2,1,0:T(8,128)S(1)} %get-tuple-element.6) | copy-start | bytes 663556
where the time goes:
time: 50 us; the launch traced here: 49.5 us
  local copies, waits for them, and re-layouts  22.9 us (46%)
  starting transfers between devices  11.9 us (24%)
  waiting for transfers between devices  6.91 us (14%)
  other arithmetic  4.04 us (8%)
  matrix products  2.62 us (5%)
  between operations  1.11 us (2%)
    unnamed x35, local copies, waits for them, and re-layouts  7.2 us
    gather x1, local copies, waits for them, and re-layouts, sample_velocity(): picked = velocity[:, corner_cells]  5.47 us
    ppermute x2, waiting for transfers between devices, padded_2(): before = lax.ppermute(last, axis, up)  4.58 us
    ppermute x2, starting transfers between devices, padded_2(): before = lax.ppermute(last, axis, up)  4.54 us
    all_to_all x1, starting transfers between devices, local(): lax.all_to_all(samples.reshape(3, peers, -1), 'gy', split_axis=1, concat_...  4.25 us
    ppermute x2, starting transfers between devices, padded_2(): after = lax.ppermute(initial, axis, down)  3.1 us
    ppermute x2, waiting for transfers between devices, padded_2(): after = lax.ppermute(initial, axis, down)  2.34 us
    scatter x2, local copies, waits for them, and re-layouts, local(): post = collide(flat.at[:, walls].set(columns), relax)  1.89 us
  transfers between devices with their start and end apart: 5, of which 3 were waited for; matrix products, arithmetic and copies ran while one was open for 8% of the time, Pallas kernels for 0%

commit v1 on v0

v1 whole, which is shorter than its diff:
```python
import functools

import jax
import jax.numpy as jnp
import numpy as np
from jax import lax
from jax.experimental import pallas as pl
from jax.experimental.pallas import tpu as pltpu
from jax.sharding import PartitionSpec as P

steps = np.array([(a - 1, b - 1, c - 1) for a in range(3) for b in range(3) for c in range(3)])
wall_ratio = (1.0 / 9.0) ** (1.0 / 7.0)
weights = np.prod(np.where(steps == 0, 2.0 / 3.0, 1.0 / 6.0), axis=1)
vander = np.array([[1.0, 1.0, 1.0], [-1.0, 0.0, 1.0], [1.0, 0.0, 1.0]])
moment = np.kron(np.kron(vander, vander), vander)
LANES = 128
MESH = pl.DeviceIdType.MESH


def equilibrium_moments():
    x, y, z = steps.T.astype(float)
    basis = np.stack(
        [
            np.ones(27),
            3 * x,
            3 * y,
            3 * z,
            4.5 * x * x - 1.5,
            4.5 * y * y - 1.5,
            4.5 * z * z - 1.5,
            9 * x * y,
            9 * x * z,
            9 * y * z,
        ],
        axis=1,
    )
    return moment @ (weights[:, None] * basis)


def forward(vals):
    for stride in (9, 3, 1):
        out = list(vals)
        for i in range(27):
            if i // stride % 3 == 0:
                lo, mid, hi = (vals[i], vals[i + stride], vals[i + 2 * stride])
                both = lo + hi
                out[i], out[i + stride], out[i + 2 * stride] = (both + mid, hi - lo, both)
        vals = out
    return vals


def plus(a, b):
    return b if a is None else a if b is None else a + b


def minus(a, b):
    return a if b is None else -b if a is None else a - b


def backward(vals):
    for stride in (9, 3, 1):
        out = list(vals)
        for i in range(27):
            if i // stride % 3 == 0:
                s0, s1, s2 = (vals[i], vals[i + stride], vals[i + 2 * stride])
                out[i], out[i + stride], out[i + 2 * stride] = (
                    minus(s2, s1),
                    minus(s0, s2),
                    plus(s2, s1),
                )
        vals = out
    return vals


def combine(terms):
    total = None
    for factor, value in terms:
        if abs(factor) < 1e-12:
            continue
        if abs(factor - 1.0) < 1e-12:
            total = plus(total, value)
        elif abs(factor + 1.0) < 1e-12:
            total = minus(total, value)
        else:
            total = plus(total, value * np.float32(factor))
    return total


def roll(value, shift, axis):
    return value if shift == 0 else pltpu.roll(value, shift % value.shape[axis], axis)


def lane_gather(row, index):
    return jnp.take_along_axis(
        jnp.broadcast_to(row, index.shape), index, axis=1, mode="promise_in_bounds"
    )


def kernel(
    devices_x,
    devices_y,
    pop_hbm,
    relax,
    solid_hbm,
    wall_hbm,
    normal_hbm,
    count,
    ref_hbm,
    stencil_hbm,
    weight_hbm,
    out,
    pop,
    solid,
    wall,
    normal,
    ref,
    stencil,
    weight,
    vel,
    samples,
    rx,
    post,
    shifted,
    stage_y,
    stage_c,
    stage_s,
    got_x,
    got_y,
    got_c,
    got_sx,
    got_sy,
    got_sc,
    masks,
    load_sem,
    send_sem,
    recv_sem,
):
    size_x, size_y = pop.shape[1:3]
    rows = size_x * size_y
    slots_all = wall.shape[2]
    slots = slots_all // devices_y
    shift_bits = slots.bit_length() - 1
    my_x = lax.axis_index("gx")
    my_y = lax.axis_index("gy")

    def at(dx, dy):
        return {
            "gx": lax.rem(my_x + (dx + devices_x), devices_x),
            "gy": lax.rem(my_y + (dy + devices_y), devices_y),
        }

    loads = [
        pltpu.make_async_copy(src, dst, load_sem.at[n])
        for n, (src, dst) in enumerate(
            [
                (pop_hbm, pop),
                (stencil_hbm, stencil),
                (weight_hbm, weight),
                (solid_hbm, solid),
                (wall_hbm, wall),
                (normal_hbm, normal),
                (ref_hbm, ref),
            ]
        )
    ]
    for load in loads:
        load.start()
    neighbours = [(dx, dy) for dx in (-1, 0, 1) for dy in (-1, 0, 1) if (dx, dy) != (0, 0)]
    greeted = neighbours + [(0, step) for step in range(2, devices_y - 1)]
    barrier = pltpu.get_barrier_semaphore()
    for dx, dy in greeted:
        pl.semaphore_signal(barrier, inc=1, device_id=at(dx, dy), device_id_type=MESH)

    sent = []

    def send(src, dst, dx, dy):
        n = len(sent)
        copy = pltpu.make_async_remote_copy(
            src_ref=src,
            dst_ref=dst,
            send_sem=send_sem.at[n],
            recv_sem=recv_sem.at[n],
            device_id=at(dx, dy),
            device_id_type=MESH,
        )
        copy.start()
        sent.append(copy)
        return copy

    loads[0].wait()
    moments, speeds = ([], [])
    for x in range(size_x):
        found = forward([pop[i, x] * np.float32(weights[i]) for i in range(27)])
        rho = found[0]
        inverse = 1.0 / rho
        u = [found[9] * inverse, found[3] * inverse, found[1] * inverse]
        for c in range(3):
            vel[c * rows + x * size_y : c * rows + (x + 1) * size_y, :] = u[c]
        moments.append(found)
        speeds.append(u)

    loads[1].wait()
    loads[2].wait()
    for tile in range(slots_all // LANES):
        lanes = slice(tile * LANES, (tile + 1) * LANES)
        cell = stencil[0, 0, :, lanes]
        lane = jnp.bitwise_and(cell, LANES - 1)
        row = jnp.right_shift(cell, 7)
        picked = [jnp.zeros(cell.shape, jnp.float32)] * 3
        for r in range(rows):
            here = row == r
            for c in range(3):
                picked[c] = jnp.where(
                    here, lane_gather(vel[c * rows + r : c * rows + r + 1, :], lane), picked[c]
                )
        factor = weight[0, 0, :, lanes]
        for c in range(3):
            samples[tile, c : c + 1, :] = jnp.sum(picked[c] * factor, axis=0, keepdims=True)
    rx[my_y] = samples[(my_y * slots) // LANES]
    pl.semaphore_wait(barrier, len(greeted))
    sample_copies = []
    for step in range(1, devices_y):
        there = lax.rem(my_y + step, devices_y)
        sample_copies.append(send(samples.at[(there * slots) // LANES], rx.at[my_y], 0, step))

    loads[3].wait()
    for side, y in ((0, size_y - 1), (1, 0)):
        for x in range(size_x):
            stage_s[side, x : x + 1, :] = solid[x, y : y + 1, :]
    solid_copies = [
        send(solid.at[size_x - 1], got_sx.at[0], 1, 0),
        send(solid.at[0], got_sx.at[1], -1, 0),
    ]
    for side, dy in ((0, 1), (1, -1)):
        solid_copies.append(send(stage_s.at[side], got_sy.at[side], 0, dy))
        solid_copies.append(send(stage_s.at[side], got_sc.at[0, side], 1, dy))
        solid_copies.append(send(stage_s.at[side], got_sc.at[1, side], -1, dy))

    coefficient = equilibrium_moments()
    for x in range(size_x):
        found, (ux, uy, uz) = (moments[x], speeds[x])
        rho, mx, my, mz = (found[0], found[9], found[3], found[1])
        basis = [rho, mx, my, mz, mx * ux, my * uy, mz * uz, mx * uy, mx * uz, my * uz]
        deviation = []
        for j in range(27):
            if j in (0, 1, 3, 9):
                deviation.append(None)
            else:
                balance = combine(list(zip(coefficient[j], basis)))
                deviation.append(minus(found[j], balance) * relax[j])
        change = backward(deviation)
        for i in range(27):
            half = 0.5 ** int(np.sum(steps[i] != 0)) / weights[i]
            post[i, x] = pop[i, x] - change[i] * np.float32(half)

    for load in loads[4:]:
        load.wait()
    cell = wall[0]
    slot = lax.broadcasted_iota(jnp.int32, (1, slots_all), 1)
    live = slot < count[0, 0]
    which = ref[0]
    offset = lax.rem(my_y * slots, LANES)
    row_hit = jnp.logical_and(
        lax.broadcasted_iota(jnp.int32, (rows, slots_all), 0) == jnp.right_shift(cell, 7), live
    )
    values = [
        jnp.right_shift(which, shift_bits) + 1,
        jnp.bitwise_and(which, slots - 1) + offset,
        jnp.right_shift(normal[0], 1),
    ]
    left = jnp.concatenate(
        [jnp.where(row_hit, value.astype(jnp.float32), 0.0) for value in values], axis=0
    ).astype(jnp.bfloat16)
    right = jnp.where(
        lax.broadcasted_iota(jnp.int32, (LANES, slots_all), 0)
        == jnp.bitwise_and(cell, LANES - 1),
        1.0,
        0.0,
    ).astype(jnp.bfloat16)
    table = lax.dot_general(
        left, right, (((1,), (1,)), ((), ())), preferred_element_type=jnp.float32
    ).astype(jnp.int32)

    for copy in sample_copies:
        copy.wait_recv()
    for x in range(size_x):
        part = [table[n * rows + x * size_y : n * rows + (x + 1) * size_y] for n in range(3)]
        source, lane, axis = part
        rho, u = (moments[x][0], speeds[x])
        new = []
        for c in range(3):
            value = jnp.zeros((size_y, LANES), jnp.float32)
            for peer in range(devices_y):
                value = jnp.where(
                    source == peer + 1, lane_gather(rx[peer, c : c + 1, :], lane), value
                )
            value = jnp.where(axis == c, 0.0, value * np.float32(wall_ratio))
            new.append(jnp.where(source > 0, value, u[c]))
        linear = [3.0 * rho * (new[c] - u[c]) for c in range(3)]
        pure = [rho * (new[c] * new[c] - u[c] * u[c]) for c in range(3)]
        rest = -1.5 * (pure[0] + pure[1] + pure[2])
        pure = [4.5 * value for value in pure]
        mixed = {
            (c, d): 9.0 * rho * (new[c] * new[d] - u[c] * u[d])
            for c, d in ((0, 1), (0, 2), (1, 2))
        }
        for i in range(14):
            step = steps[i]
            used = [c for c in range(3) if step[c] != 0]
            even, odd = (rest, None)
            for c in used:
                even = even + pure[c]
                odd = plus(odd, linear[c]) if step[c] > 0 else minus(odd, linear[c])
            for c, d in mixed:
                if step[c] * step[d] > 0:
                    even = even + mixed[c, d]
                elif step[c] * step[d] < 0:
                    even = even - mixed[c, d]
            if odd is None:
                post[i, x] = post[i, x] + even
            else:
                post[i, x] = post[i, x] + (even + odd)
                post[26 - i, x] = post[26 - i, x] + (even - odd)
        for i in range(27):
            a, b, c = steps[i]
            value = roll(roll(post[i, x], b, 0), c, 1)
            shifted[i, x] = value
            if b != 0:
                side = 0 if b > 0 else 1
                edge = 0 if b > 0 else size_y - 1
                line = value[edge : edge + 1, :]
                if 0 <= x + a < size_x:
                    n = ((a + 1) * 3 + c + 1) * size_x + x
                    stage_y[side, n : n + 1, :] = line
                else:
                    stage_c[0 if a > 0 else 1, side, c + 1 : c + 2, :] = line

    halo = [
        send(shifted.at[18:27, size_x - 1], got_x.at[0], 1, 0),
        send(shifted.at[0:9, 0], got_x.at[1], -1, 0),
    ]
    for side, dy in ((0, 1), (1, -1)):
        for way, dx in ((0, 1), (1, -1)):
            halo.append(send(stage_c.at[way, side], got_c.at[way, side], dx, dy))
    for side, dy in ((0, 1), (1, -1)):
        halo.append(send(stage_y.at[side], got_y.at[side], 0, dy))

    for copy in solid_copies:
        copy.wait_recv()
    line_of = lax.broadcasted_iota(jnp.int32, (size_y, LANES), 0)

    def mend(value, line, b):
        edge = 0 if b > 0 else size_y - 1
        return jnp.where(line_of == edge, jnp.broadcast_to(line, value.shape), value)

    for x in range(-1, size_x + 1):
        plane = got_sx[0] if x < 0 else got_sx[1] if x == size_x else solid[x]
        for b in (-1, 0, 1):
            value = roll(plane, b, 0)
            if b != 0:
                side = 0 if b > 0 else 1
                if x < 0:
                    line = got_sc[0, side, size_x - 1 : size_x, :]
                elif x == size_x:
                    line = got_sc[1, side, 0:1, :]
                else:
                    line = got_sy[side, x : x + 1, :]
                value = mend(value, line, b)
            for c in (-1, 0, 1):
                masks[(b + 1) * 3 + c + 1, x + 1] = roll(value, c, 1)

    for copy in halo:
        copy.wait_recv()
    for i in range(27):
        a, b, c = steps[i]
        way = 0 if a > 0 else 1
        side = 0 if b > 0 else 1
        for x in range(size_x):
            origin = x - a
            if 0 <= origin < size_x:
                value = shifted[i, origin]
                n = ((a + 1) * 3 + c + 1) * size_x + origin
                line = got_y[side, n : n + 1, :] if b != 0 else None
            else:
                value = got_x[way, i % 9]
                line = got_c[way, side, c + 1 : c + 2, :] if b != 0 else None
            if b != 0:
                value = mend(value, line, b)
            blocked = masks[(b + 1) * 3 + c + 1, origin + 1] != 0
            out[i, x] = jnp.where(blocked, post[26 - i, x], value)
    for copy in sent:
        copy.wait_send()


def local(populations, relax, solid, wall_cell, wall_normal, wall_count, sample_ref, cells, factors):
    devices_x, devices_y = (lax.axis_size("gx"), lax.axis_size("gy"))
    size_x, size_y, size_z = populations.shape[1:]
    slots_all = wall_cell.shape[2]
    slots = slots_all // devices_y
    assert size_z == LANES and LANES % slots == 0 and slots & (slots - 1) == 0
    assert slots_all % LANES == 0 and devices_x > 2 and devices_y > 2
    f32, i32 = (jnp.float32, jnp.int32)
    lines = -(-9 * size_x // 8) * 8
    sends = devices_y - 1 + 16
    vmem = pltpu.VMEM
    tile = (size_y, LANES)
    anywhere = pl.BlockSpec(memory_space=pl.ANY)
    smem = pl.BlockSpec(memory_space=pltpu.SMEM)
    return pl.pallas_call(
        functools.partial(kernel, devices_x, devices_y),
        out_shape=jax.ShapeDtypeStruct(populations.shape, f32),
        in_specs=[
            anywhere,
            smem,
            anywhere,
            anywhere,
            anywhere,
            smem,
            anywhere,
            anywhere,
            anywhere,
        ],
        out_specs=pl.BlockSpec(memory_space=pltpu.VMEM),
        scratch_shapes=[
            vmem(populations.shape, f32),
            vmem(solid.shape, i32),
            vmem(wall_cell.shape, i32),
            vmem(wall_normal.shape, i32),
            vmem(sample_ref.shape, i32),
            vmem(cells.shape, i32),
            vmem(factors.shape, f32),
            vmem((3 * size_x * size_y, LANES), f32),
            vmem((slots_all // LANES, 8, LANES), f32),
            vmem((devices_y, 8, LANES), f32),
            vmem(populations.shape, f32),
            vmem(populations.shape, f32),
            vmem((2, lines, LANES), f32),
            vmem((2, 2, 8, LANES), f32),
            vmem((2, 8, LANES), i32),
            vmem((2, 9) + tile, f32),
            vmem((2, lines, LANES), f32),
            vmem((2, 2, 8, LANES), f32),
            vmem((2,) + tile, i32),
            vmem((2, 8, LANES), i32),
            vmem((2, 2, 8, LANES), i32),
            vmem((9, size_x + 2) + tile, i32),
            pltpu.SemaphoreType.DMA((7,)),
            pltpu.SemaphoreType.DMA((sends,)),
            pltpu.SemaphoreType.DMA((sends,)),
        ],
        compiler_params=pltpu.CompilerParams(collective_id=0, has_side_effects=True),
        name="lattice_step",
    )(populations, relax, solid, wall_cell, wall_normal, wall_count, sample_ref, cells, factors)


def solution(mesh):
    return jax.shard_map(
        local,
        mesh=mesh,
        in_specs=(
            P(None, "gx", "gy", None),
            P(),
            P("gx", "gy", None),
            P("gx", "gy", None),
            P("gx", "gy", None),
            P("gx", "gy"),
            P("gx", "gy", None),
            P("gx", "gy", None, None),
            P("gx", "gy", None, None),
        ),
        out_specs=P(None, "gx", "gy", None),
        check_vma=False,
    )
```

time: 50 us -> 16.8 us (0.34)
  the two profiles are of different devices: /device:TPU:1 before, /device:TPU:0 now
where the time goes in v1:
time: 16.8 us; the launch traced here: 16.6 us
  Pallas kernels  14.3 us (85%)
  local copies, waits for them, and re-layouts  1.64 us (10%)
  between operations  0.66 us (4%)
    pallas_call x1, Pallas kernels, local(): pl.pallas_call(functools.partial(kernel, devices_x, devices_y), out_shape...  14.3 us
    unnamed x1, local copies, waits for them, and re-layouts  1.64 us

profile of v1, /device:TPU:0, one launch (start us, length us, event | category | flops | bytes accessed | tf_op | source)
XLA Modules:
  0.0 16.6 jit_solution(7729961575154599055)
XLA Ops:
  0.7 14.3 %lattice_step.1 = f32[27,2,8,128]{3,2,1,0:T(8,128)} custom-call(f32[27,2,8,128]{3,2,1,0:T(8,128)} %pop_hbm.1, f32[27]{0:T(128)} %relax.1, s32[2,8,128]{2,1,0:T(8,128)} %solid_hbm.1, s32[1,1,256]{2,1,0:T(1,128)} %wall_hbm.1, s32[1,1,256]{2,1,0:T(1,128)} %normal_hbm.1, s32[1,1]{1,0:T(1,128)S(6)} %copy.11.count, s32[1,1,256]{2,1,0:T(1,128)} %ref_hbm.1, ...), custom_call_target="tpu_custom_call" | custom-call | tf_op jit(solution)/shard_map/lattice_step/pallas_call | solution.py:409
  15.0 1.6 %copy.12 = f32[27,2,8,128]{3,2,1,0:T(8,128)} copy(f32[27,2,8,128]{3,2,1,0:T(8,128)} %lattice_step.1) | data formatting | bytes 442368

commit v2 on v1

--- a/solution.py
+++ b/solution.py
@@ -120,16 +120,30 @@
     samples,
     rx,
     post,
+    settled,
+    fields,
+    fresh,
     shifted,
     stage_y,
     stage_c,
     stage_s,
+    stage_f,
+    stage_n,
     got_x,
     got_y,
     got_c,
     got_sx,
     got_sy,
     got_sc,
+    got_fx,
+    got_fy,
+    got_fc,
+    got_nx,
+    got_ny,
+    got_nc,
+    lines,
+    line_fields,
+    line_fresh,
     masks,
     load_sem,
     send_sem,
@@ -196,6 +210,8 @@
         u = [found[9] * inverse, found[3] * inverse, found[1] * inverse]
         for c in range(3):
             vel[c * rows + x * size_y : c * rows + (x + 1) * size_y, :] = u[c]
+        for f, value in enumerate([rho] + u):
+            fields[f, x] = value
         moments.append(found)
         speeds.append(u)
 
@@ -252,6 +268,37 @@
         for i in range(27):
             half = 0.5 ** int(np.sum(steps[i] != 0)) / weights[i]
             post[i, x] = pop[i, x] - change[i] * np.float32(half)
+
+    for i in range(27):
+        a, b, c = steps[i]
+        if b == 0:
+            continue
+        side = 0 if b > 0 else 1
+        edge = size_y - 1 if b > 0 else 0
+        for x in range(size_x):
+            line = post[i, x, edge : edge + 1, :]
+            if 0 <= x + a < size_x:
+                n = ((a + 1) * 3 + c + 1) * size_x + x
+                stage_y[side, n : n + 1, :] = line
+            else:
+                stage_c[0 if a > 0 else 1, side, c + 1 : c + 2, :] = line
+    for side, y in ((0, size_y - 1), (1, 0)):
+        for f in range(4):
+            for x in range(size_x):
+                n = f * size_x + x
+                stage_f[side, n : n + 1, :] = fields[f, x, y : y + 1, :]
+    early = [
+        send(post.at[18:27, size_x - 1], got_x.at[0], 1, 0),
+        send(post.at[0:9, 0], got_x.at[1], -1, 0),
+        send(fields.at[:, size_x - 1], got_fx.at[0], 1, 0),
+        send(fields.at[:, 0], got_fx.at[1], -1, 0),
+    ]
+    for side, dy in ((0, 1), (1, -1)):
+        for way, dx in ((0, 1), (1, -1)):
+            early.append(send(stage_c.at[way, side], got_c.at[way, side], dx, dy))
+            early.append(send(stage_f.at[side], got_fc.at[way, side], dx, dy))
+        early.append(send(stage_y.at[side], got_y.at[side], 0, dy))
+        early.append(send(stage_f.at[side], got_fy.at[side], 0, dy))
 
     for load in loads[4:]:
         load.wait()
@@ -286,8 +333,6 @@
     for x in range(size_x):
         part = [table[n * rows + x * size_y : n * rows + (x + 1) * size_y] for n in range(3)]
         source, lane, axis = part
-        rho, u = (moments[x][0], speeds[x])
-        new = []
         for c in range(3):
             value = jnp.zeros((size_y, LANES), jnp.float32)
             for peer in range(devices_y):
@@ -295,7 +340,22 @@
                     source == peer + 1, lane_gather(rx[peer, c : c + 1, :], lane), value
                 )
             value = jnp.where(axis == c, 0.0, value * np.float32(wall_ratio))
-            new.append(jnp.where(source > 0, value, u[c]))
+            value = jnp.where(source > 0, value, speeds[x][c])
+            fresh[c, x] = value
+            for side, y in ((0, size_y - 1), (1, 0)):
+                n = c * size_x + x
+                stage_n[side, n : n + 1, :] = value[y : y + 1, :]
+    late = [
+        send(fresh.at[:, size_x - 1], got_nx.at[0], 1, 0),
+        send(fresh.at[:, 0], got_nx.at[1], -1, 0),
+    ]
+    for side, dy in ((0, 1), (1, -1)):
+        late.append(send(stage_n.at[side], got_nc.at[0, side], 1, dy))
+        late.append(send(stage_n.at[side], got_nc.at[1, side], -1, dy))
+    for side, dy in ((0, 1), (1, -1)):
+        late.append(send(stage_n.at[side], got_ny.at[side], 0, dy))
+
+    def correction(rho, u, new, wanted):
         linear = [3.0 * rho * (new[c] - u[c]) for c in range(3)]
         pure = [rho * (new[c] * new[c] - u[c] * u[c]) for c in range(3)]
         rest = -1.5 * (pure[0] + pure[1] + pure[2])
@@ -304,46 +364,35 @@
             (c, d): 9.0 * rho * (new[c] * new[d] - u[c] * u[d])
             for c, d in ((0, 1), (0, 2), (1, 2))
         }
-        for i in range(14):
-            step = steps[i]
-            used = [c for c in range(3) if step[c] != 0]
-            even, odd = (rest, None)
-            for c in used:
-                even = even + pure[c]
-                odd = plus(odd, linear[c]) if step[c] > 0 else minus(odd, linear[c])
-            for c, d in mixed:
-                if step[c] * step[d] > 0:
-                    even = even + mixed[c, d]
-                elif step[c] * step[d] < 0:
-                    even = even - mixed[c, d]
-            if odd is None:
-                post[i, x] = post[i, x] + even
-            else:
-                post[i, x] = post[i, x] + (even + odd)
-                post[26 - i, x] = post[26 - i, x] + (even - odd)
+        halves, found = ({}, {})
+        for i in wanted:
+            first = min(i, 26 - i)
+            if first not in halves:
+                step = steps[first]
+                even, odd = (rest, None)
+                for c in range(3):
+                    if step[c] != 0:
+                        even = even + pure[c]
+                        odd = plus(odd, linear[c]) if step[c] > 0 else minus(odd, linear[c])
+                for c, d in mixed:
+                    if step[c] * step[d] > 0:
+                        even = even + mixed[c, d]
+                    elif step[c] * step[d] < 0:
+                        even = even - mixed[c, d]
+                halves[first] = (even, odd)
+            even, odd = halves[first]
+            found[i] = even if odd is None else even + odd if i == first else even - odd
+        return found
+
+    for x in range(size_x):
+        found = correction(
+            fields[0, x], [fields[1 + c, x] for c in range(3)], [fresh[c, x] for c in range(3)], range(27)
+        )
         for i in range(27):
             a, b, c = steps[i]
-            value = roll(roll(post[i, x], b, 0), c, 1)
-            shifted[i, x] = value
-            if b != 0:
-                side = 0 if b > 0 else 1
-                edge = 0 if b > 0 else size_y - 1
-                line = value[edge : edge + 1, :]
-                if 0 <= x + a < size_x:
-                    n = ((a + 1) * 3 + c + 1) * size_x + x
-                    stage_y[side, n : n + 1, :] = line
-                else:
-                    stage_c[0 if a > 0 else 1, side, c + 1 : c + 2, :] = line
-
-    halo = [
-        send(shifted.at[18:27, size_x - 1], got_x.at[0], 1, 0),
-        send(shifted.at[0:9, 0], got_x.at[1], -1, 0),
-    ]
-    for side, dy in ((0, 1), (1, -1)):
-        for way, dx in ((0, 1), (1, -1)):
-            halo.append(send(stage_c.at[way, side], got_c.at[way, side], dx, dy))
-    for side, dy in ((0, 1), (1, -1)):
-        halo.append(send(stage_y.at[side], got_y.at[side], 0, dy))
+            value = post[i, x] + found[i]
+            settled[i, x] = value
+            shifted[i, x] = roll(roll(value, b, 0), c, 1)
 
     for copy in solid_copies:
         copy.wait_recv()
@@ -369,27 +418,83 @@
             for c in (-1, 0, 1):
                 masks[(b + 1) * 3 + c + 1, x + 1] = roll(value, c, 1)
 
-    for copy in halo:
+    def gather_rows(target, index, straight, corner, f):
+        for x in range(size_x):
+            n = f * size_x + x
+            target[index + (slice(x, x + 1),)] = straight[n : n + 1, :]
+        n = f * size_x + size_x - 1
+        target[index + (slice(size_x, size_x + 1),)] = corner[0][n : n + 1, :]
+        n = f * size_x
+        target[index + (slice(size_x + 1, size_x + 2),)] = corner[1][n : n + 1, :]
+
+    for copy in early:
         copy.wait_recv()
+    for side in range(2):
+        for j in range(9):
+            a, c = (j // 3 - 1, j % 3 - 1)
+            for x in range(size_x):
+                if 0 <= x + a < size_x:
+                    n = j * size_x + x
+                    lines[side, j, x : x + 1, :] = got_y[side, n : n + 1, :]
+            if a != 0:
+                way = 0 if a > 0 else 1
+                lines[side, j, size_x + way : size_x + way + 1, :] = got_c[
+                    way, side, c + 1 : c + 2, :
+                ]
+        for f in range(4):
+            gather_rows(
+                line_fields, (side, f), got_fy.at[side], [got_fc.at[way, side] for way in (0, 1)], f
+            )
+
+    for copy in late:
+        copy.wait_recv()
+    border = {}
+    for side, b in ((0, 1), (1, -1)):
+        for c in range(3):
+            gather_rows(
+                line_fresh, (side, c), got_ny.at[side], [got_nc.at[way, side] for way in (0, 1)], c
+            )
+        wanted = [i for i in range(27) if steps[i][1] == b]
+        found = correction(
+            line_fields[side, 0],
+            [line_fields[side, 1 + c] for c in range(3)],
+            [line_fresh[side, c] for c in range(3)],
+            wanted,
+        )
+        for i in wanted:
+            a, _, c = steps[i]
+            border[i] = roll(lines[side, (a + 1) * 3 + c + 1] + found[i], c, 1)
+    planes = {}
+    for way, a in ((0, 1), (1, -1)):
+        wanted = [i for i in range(27) if steps[i][0] == a]
+        found = correction(
+            got_fx[way, 0],
+            [got_fx[way, 1 + c] for c in range(3)],
+            [got_nx[way, c] for c in range(3)],
+            wanted,
+        )
+        for i in wanted:
+            _, b, c = steps[i]
+            planes[i] = roll(roll(got_x[way, i % 9] + found[i], b, 0), c, 1)
     for i in range(27):
         a, b, c = steps[i]
-        way = 0 if a > 0 else 1
-        side = 0 if b > 0 else 1
         for x in range(size_x):
             origin = x - a
-            if 0 <= origin < size_x:
-                value = shifted[i, origin]
-                n = ((a + 1) * 3 + c + 1) * size_x + origin
-                line = got_y[side, n : n + 1, :] if b != 0 else None
-            else:
-                value = got_x[way, i % 9]
-                line = got_c[way, side, c + 1 : c + 2, :] if b != 0 else None
+            inside = 0 <= origin < size_x
+            value = shifted[i, origin] if inside else planes[i]
             if b != 0:
-                value = mend(value, line, b)
+                n = origin if inside else size_x + (0 if a > 0 else 1)
+                value = mend(value, border[i][n : n + 1, :], b)
             blocked = masks[(b + 1) * 3 + c + 1, origin + 1] != 0
-            out[i, x] = jnp.where(blocked, post[26 - i, x], value)
+            out[i, x] = jnp.where(blocked, settled[26 - i, x], value)
     for copy in sent:
         copy.wait_send()
+
+
+def write_out(source, out, sem):
+    copy = pltpu.make_async_copy(source, out, sem)
+    copy.start()
+    copy.wait()
 
 
 def local(populations, relax, solid, wall_cell, wall_normal, wall_count, sample_ref, cells, factors):
@@ -401,14 +506,16 @@
     assert slots_all % LANES == 0 and devices_x > 2 and devices_y > 2
     f32, i32 = (jnp.float32, jnp.int32)
     lines = -(-9 * size_x // 8) * 8
-    sends = devices_y - 1 + 16
+    assert size_x + 2 <= 8
+    few = -(-4 * size_x // 8) * 8
+    sends = devices_y - 1 + 8 + 16 + 8
     vmem = pltpu.VMEM
     tile = (size_y, LANES)
     anywhere = pl.BlockSpec(memory_space=pl.ANY)
     smem = pl.BlockSpec(memory_space=pltpu.SMEM)
-    return pl.pallas_call(
+    result = pl.pallas_call(
         functools.partial(kernel, devices_x, devices_y),
-        out_shape=jax.ShapeDtypeStruct(populations.shape, f32),
+        out_shape=pltpu.VMEM(populations.shape, f32),
         in_specs=[
             anywhere,
             smem,
@@ -434,15 +541,29 @@
             vmem((devices_y, 8, LANES), f32),
             vmem(populations.shape, f32),
             vmem(populations.shape, f32),
+            vmem((4, size_x) + tile, f32),
+            vmem((3, size_x) + tile, f32),
+            vmem(populations.shape, f32),
             vmem((2, lines, LANES), f32),
             vmem((2, 2, 8, LANES), f32),
             vmem((2, 8, LANES), i32),
+            vmem((2, few, LANES), f32),
+            vmem((2, few, LANES), f32),
             vmem((2, 9) + tile, f32),
             vmem((2, lines, LANES), f32),
             vmem((2, 2, 8, LANES), f32),
             vmem((2,) + tile, i32),
             vmem((2, 8, LANES), i32),
             vmem((2, 2, 8, LANES), i32),
+            vmem((2, 4) + tile, f32),
+            vmem((2, few, LANES), f32),
+            vmem((2, 2, few, LANES), f32),
+            vmem((2, 3) + tile, f32),
+            vmem((2, few, LANES), f32),
+            vmem((2, 2, few, LANES), f32),
+            vmem((2, 9, 8, LANES), f32),
+            vmem((2, 4, 8, LANES), f32),
+            vmem((2, 3, 8, LANES), f32),
             vmem((9, size_x + 2) + tile, i32),
             pltpu.SemaphoreType.DMA((7,)),
             pltpu.SemaphoreType.DMA((sends,)),
@@ -451,6 +572,15 @@
         compiler_params=pltpu.CompilerParams(collective_id=0, has_side_effects=True),
         name="lattice_step",
     )(populations, relax, solid, wall_cell, wall_normal, wall_count, sample_ref, cells, factors)
+    result = pltpu.with_memory_space_constraint(result, pltpu.VMEM)
+    return pl.pallas_call(
+        write_out,
+        out_shape=jax.ShapeDtypeStruct(populations.shape, f32),
+        in_specs=[pl.BlockSpec(memory_space=pltpu.VMEM)],
+        out_specs=anywhere,
+        scratch_shapes=[pltpu.SemaphoreType.DMA],
+        name="write_out",
+    )(result)
 
 
 def solution(mesh):

time: 16.8 us -> 15.1 us (0.90)
  local copies, waits for them, and re-layouts: 1.64 us -> 0 us
    unnamed x1 -> x0, local copies, waits for them, and re-layouts: 1.64 us -> none
    pallas_call x0 -> x1, Pallas kernels: none -> 0.7 us  [local(): pl.pallas_call(write_out, out_shape=jax.ShapeDtypeStruct(populations.shap...]
    pallas_call x1, Pallas kernels: 14.3 us -> 13.6 us  [local(): pl.pallas_call(functools.partial(kernel, devices_x, devices_y), out_shape...]
where the time goes in v2:
time: 15.1 us; the launch traced here: 15 us
  Pallas kernels  14.3 us (95%)
  between operations  0.66 us (4%)
    pallas_call x1, Pallas kernels, local(): pl.pallas_call(functools.partial(kernel, devices_x, devices_y), out_shape...  13.6 us
    pallas_call x1, Pallas kernels, local(): pl.pallas_call(write_out, out_shape=jax.ShapeDtypeStruct(populations.shap...  0.7 us

profile of v2, /device:TPU:0, one launch (start us, length us, event | category | flops | bytes accessed | tf_op | source)
XLA Modules:
  0.0 15.0 jit_solution(7830922446614321337)
XLA Ops:
  0.7 13.6 %lattice_step.1.source = f32[27,2,8,128]{3,2,1,0:T(8,128)S(1)} custom-call(f32[27,2,8,128]{3,2,1,0:T(8,128)} %pop_hbm.1, f32[27]{0:T(128)} %relax.1, s32[2,8,128]{2,1,0:T(8,128)} %solid_hbm.1, s32[1,1,256]{2,1,0:T(1,128)} %wall_hbm.1, s32[1,1,256]{2,1,0:T(1,128)} %normal_hbm.1, s32[1,1]{1,0:T(1,128)S(6)} %copy.10.count, s32[1,1,256]{2,1,0:T(1,128)} %ref_hbm.1, ...), custom_call_target="tpu_custom_call" | custom-call | tf_op jit(solution)/shard_map/lattice_step/pallas_call | solution.py:516
  14.3 0.7 %write_out.1 = f32[27,2,8,128]{3,2,1,0:T(8,128)} custom-call(f32[27,2,8,128]{3,2,1,0:T(8,128)S(1)} %lattice_step.1.source), custom_call_target="tpu_custom_call" | custom-call | tf_op jit(solution)/shard_map/write_out/pallas_call | solution.py:576

commit v3 on v2

--- a/solution.py
+++ b/solution.py
@@ -122,13 +122,11 @@
     post,
     settled,
     fields,
-    fresh,
     shifted,
     stage_y,
     stage_c,
     stage_s,
     stage_f,
-    stage_n,
     got_x,
     got_y,
     got_c,
@@ -138,12 +136,8 @@
     got_fx,
     got_fy,
     got_fc,
-    got_nx,
-    got_ny,
-    got_nc,
     lines,
     line_fields,
-    line_fresh,
     masks,
     load_sem,
     send_sem,
@@ -179,8 +173,7 @@
     ]
     for load in loads:
         load.start()
-    neighbours = [(dx, dy) for dx in (-1, 0, 1) for dy in (-1, 0, 1) if (dx, dy) != (0, 0)]
-    greeted = neighbours + [(0, step) for step in range(2, devices_y - 1)]
+    greeted = [(dx, dy) for dx in (-1, 0, 1) for dy in range(devices_y) if (dx, dy) != (0, 0)]
     barrier = pltpu.get_barrier_semaphore()
     for dx, dy in greeted:
         pl.semaphore_signal(barrier, inc=1, device_id=at(dx, dy), device_id_type=MESH)
@@ -231,13 +224,11 @@
                 )
         factor = weight[0, 0, :, lanes]
         for c in range(3):
-            samples[tile, c : c + 1, :] = jnp.sum(picked[c] * factor, axis=0, keepdims=True)
-    rx[my_y] = samples[(my_y * slots) // LANES]
+            n = tile * 3 + c
+            samples[n : n + 1, :] = jnp.sum(picked[c] * factor, axis=0, keepdims=True)
+    rx[1, my_y] = samples[...]
     pl.semaphore_wait(barrier, len(greeted))
-    sample_copies = []
-    for step in range(1, devices_y):
-        there = lax.rem(my_y + step, devices_y)
-        sample_copies.append(send(samples.at[(there * slots) // LANES], rx.at[my_y], 0, step))
+    sample_copies = [send(samples, rx.at[1 - dx, my_y], dx, dy) for dx, dy in greeted]
 
     loads[3].wait()
     for side, y in ((0, size_y - 1), (1, 0)):
@@ -268,37 +259,6 @@
         for i in range(27):
             half = 0.5 ** int(np.sum(steps[i] != 0)) / weights[i]
             post[i, x] = pop[i, x] - change[i] * np.float32(half)
-
-    for i in range(27):
-        a, b, c = steps[i]
-        if b == 0:
-            continue
-        side = 0 if b > 0 else 1
-        edge = size_y - 1 if b > 0 else 0
-        for x in range(size_x):
-            line = post[i, x, edge : edge + 1, :]
-            if 0 <= x + a < size_x:
-                n = ((a + 1) * 3 + c + 1) * size_x + x
-                stage_y[side, n : n + 1, :] = line
-            else:
-                stage_c[0 if a > 0 else 1, side, c + 1 : c + 2, :] = line
-    for side, y in ((0, size_y - 1), (1, 0)):
-        for f in range(4):
-            for x in range(size_x):
-                n = f * size_x + x
-                stage_f[side, n : n + 1, :] = fields[f, x, y : y + 1, :]
-    early = [
-        send(post.at[18:27, size_x - 1], got_x.at[0], 1, 0),
-        send(post.at[0:9, 0], got_x.at[1], -1, 0),
-        send(fields.at[:, size_x - 1], got_fx.at[0], 1, 0),
-        send(fields.at[:, 0], got_fx.at[1], -1, 0),
-    ]
-    for side, dy in ((0, 1), (1, -1)):
-        for way, dx in ((0, 1), (1, -1)):
-            early.append(send(stage_c.at[way, side], got_c.at[way, side], dx, dy))
-            early.append(send(stage_f.at[side], got_fc.at[way, side], dx, dy))
-        early.append(send(stage_y.at[side], got_y.at[side], 0, dy))
-        early.append(send(stage_f.at[side], got_fy.at[side], 0, dy))
 
     for load in loads[4:]:
         load.wait()
@@ -326,34 +286,63 @@
     ).astype(jnp.bfloat16)
     table = lax.dot_general(
         left, right, (((1,), (1,)), ((), ())), preferred_element_type=jnp.float32
-    ).astype(jnp.int32)
+    )
+    for n in range(3):
+        for x in range(size_x):
+            first = n * rows + x * size_y
+            fields[4 + n, x] = table[first : first + size_y]
+
+    for i in range(27):
+        a, b, c = steps[i]
+        if b == 0:
+            continue
+        side = 0 if b > 0 else 1
+        edge = size_y - 1 if b > 0 else 0
+        for x in range(size_x):
+            line = post[i, x, edge : edge + 1, :]
+            if 0 <= x + a < size_x:
+                n = ((a + 1) * 3 + c + 1) * size_x + x
+                stage_y[side, n : n + 1, :] = line
+            else:
+                stage_c[0 if a > 0 else 1, side, c + 1 : c + 2, :] = line
+    for side, y in ((0, size_y - 1), (1, 0)):
+        for f in range(7):
+            for x in range(size_x):
+                n = f * size_x + x
+                stage_f[side, n : n + 1, :] = fields[f, x, y : y + 1, :]
+    early = [
+        send(post.at[18:27, size_x - 1], got_x.at[0], 1, 0),
+        send(post.at[0:9, 0], got_x.at[1], -1, 0),
+        send(fields.at[:, size_x - 1], got_fx.at[0], 1, 0),
+        send(fields.at[:, 0], got_fx.at[1], -1, 0),
+    ]
+    for side, dy in ((0, 1), (1, -1)):
+        for way, dx in ((0, 1), (1, -1)):
+            early.append(send(stage_c.at[way, side], got_c.at[way, side], dx, dy))
+            early.append(send(stage_f.at[side], got_fc.at[way, side], dx, dy))
+        early.append(send(stage_y.at[side], got_y.at[side], 0, dy))
+        early.append(send(stage_f.at[side], got_fy.at[side], 0, dy))
 
     for copy in sample_copies:
         copy.wait_recv()
-    for x in range(size_x):
-        part = [table[n * rows + x * size_y : n * rows + (x + 1) * size_y] for n in range(3)]
-        source, lane, axis = part
+
+    def velocity(field, owner, groups):
+        source, lane, axis = [value.astype(jnp.int32) for value in field[4:]]
+        lane = jnp.bitwise_and(lane, LANES - 1)
+        tile = (owner * slots) // LANES
+        new = []
         for c in range(3):
             value = jnp.zeros((size_y, LANES), jnp.float32)
-            for peer in range(devices_y):
-                value = jnp.where(
-                    source == peer + 1, lane_gather(rx[peer, c : c + 1, :], lane), value
-                )
+            for group, mask in groups:
+                for peer in range(devices_y):
+                    here = source == peer + 1
+                    if mask is not None:
+                        here = jnp.logical_and(here, mask)
+                    line = rx[group, peer, pl.ds(tile * 3 + c, 1), :]
+                    value = jnp.where(here, lane_gather(line, lane), value)
             value = jnp.where(axis == c, 0.0, value * np.float32(wall_ratio))
-            value = jnp.where(source > 0, value, speeds[x][c])
-            fresh[c, x] = value
-            for side, y in ((0, size_y - 1), (1, 0)):
-                n = c * size_x + x
-                stage_n[side, n : n + 1, :] = value[y : y + 1, :]
-    late = [
-        send(fresh.at[:, size_x - 1], got_nx.at[0], 1, 0),
-        send(fresh.at[:, 0], got_nx.at[1], -1, 0),
-    ]
-    for side, dy in ((0, 1), (1, -1)):
-        late.append(send(stage_n.at[side], got_nc.at[0, side], 1, dy))
-        late.append(send(stage_n.at[side], got_nc.at[1, side], -1, dy))
-    for side, dy in ((0, 1), (1, -1)):
-        late.append(send(stage_n.at[side], got_ny.at[side], 0, dy))
+            new.append(jnp.where(source > 0, value, field[1 + c]))
+        return new
 
     def correction(rho, u, new, wanted):
         linear = [3.0 * rho * (new[c] - u[c]) for c in range(3)]
@@ -385,9 +374,8 @@
         return found
 
     for x in range(size_x):
-        found = correction(
-            fields[0, x], [fields[1 + c, x] for c in range(3)], [fresh[c, x] for c in range(3)], range(27)
-        )
+        field = [fields[f, x] for f in range(7)]
+        found = correction(field[0], field[1:4], velocity(field, my_y, [(1, None)]), range(27))
         for i in range(27):
             a, b, c = steps[i]
             value = post[i, x] + found[i]
@@ -441,37 +429,27 @@
                 lines[side, j, size_x + way : size_x + way + 1, :] = got_c[
                     way, side, c + 1 : c + 2, :
                 ]
-        for f in range(4):
+        for f in range(7):
             gather_rows(
                 line_fields, (side, f), got_fy.at[side], [got_fc.at[way, side] for way in (0, 1)], f
             )
 
-    for copy in late:
-        copy.wait_recv()
     border = {}
     for side, b in ((0, 1), (1, -1)):
-        for c in range(3):
-            gather_rows(
-                line_fresh, (side, c), got_ny.at[side], [got_nc.at[way, side] for way in (0, 1)], c
-            )
         wanted = [i for i in range(27) if steps[i][1] == b]
-        found = correction(
-            line_fields[side, 0],
-            [line_fields[side, 1 + c] for c in range(3)],
-            [line_fresh[side, c] for c in range(3)],
-            wanted,
-        )
+        field = [line_fields[side, f] for f in range(7)]
+        owner = lax.rem(my_y + (devices_y - b), devices_y)
+        groups = [(1, line_of < size_x), (0, line_of == size_x), (2, line_of == size_x + 1)]
+        found = correction(field[0], field[1:4], velocity(field, owner, groups), wanted)
         for i in wanted:
             a, _, c = steps[i]
             border[i] = roll(lines[side, (a + 1) * 3 + c + 1] + found[i], c, 1)
     planes = {}
     for way, a in ((0, 1), (1, -1)):
         wanted = [i for i in range(27) if steps[i][0] == a]
+        field = [got_fx[way, f] for f in range(7)]
         found = correction(
-            got_fx[way, 0],
-            [got_fx[way, 1 + c] for c in range(3)],
-            [got_nx[way, c] for c in range(3)],
-            wanted,
+            field[0], field[1:4], velocity(field, my_y, [(0 if a > 0 else 2, None)]), wanted
         )
         for i in wanted:
             _, b, c = steps[i]
@@ -506,9 +484,10 @@
     assert slots_all % LANES == 0 and devices_x > 2 and devices_y > 2
     f32, i32 = (jnp.float32, jnp.int32)
     lines = -(-9 * size_x // 8) * 8
-    assert size_x + 2 <= 8
-    few = -(-4 * size_x // 8) * 8
-    sends = devices_y - 1 + 8 + 16 + 8
+    assert size_x + 2 <= size_y == 8
+    few = -(-7 * size_x // 8) * 8
+    held = -(-3 * slots_all // LANES // 8) * 8
+    sends = 3 * devices_y - 1 + 8 + 16
     vmem = pltpu.VMEM
     tile = (size_y, LANES)
     anywhere = pl.BlockSpec(memory_space=pl.ANY)
@@ -537,17 +516,15 @@
             vmem(cells.shape, i32),
             vmem(factors.shape, f32),
             vmem((3 * size_x * size_y, LANES), f32),
-            vmem((slots_all // LANES, 8, LANES), f32),
-            vmem((devices_y, 8, LANES), f32),
+            vmem((held, LANES), f32),
+            vmem((3, devices_y, held, LANES), f32),
             vmem(populations.shape, f32),
             vmem(populations.shape, f32),
-            vmem((4, size_x) + tile, f32),
-            vmem((3, size_x) + tile, f32),
+            vmem((7, size_x) + tile, f32),
             vmem(populations.shape, f32),
             vmem((2, lines, LANES), f32),
             vmem((2, 2, 8, LANES), f32),
             vmem((2, 8, LANES), i32),
-            vmem((2, few, LANES), f32),
             vmem((2, few, LANES), f32),
             vmem((2, 9) + tile, f32),
             vmem((2, lines, LANES), f32),
@@ -555,15 +532,11 @@
             vmem((2,) + tile, i32),
             vmem((2, 8, LANES), i32),
             vmem((2, 2, 8, LANES), i32),
-            vmem((2, 4) + tile, f32),
-            vmem((2, few, LANES), f32),
-            vmem((2, 2, few, LANES), f32),
-            vmem((2, 3) + tile, f32),
+            vmem((2, 7) + tile, f32),
             vmem((2, few, LANES), f32),
             vmem((2, 2, few, LANES), f32),
             vmem((2, 9, 8, LANES), f32),
-            vmem((2, 4, 8, LANES), f32),
-            vmem((2, 3, 8, LANES), f32),
+            vmem((2, 7, 8, LANES), f32),
             vmem((9, size_x + 2) + tile, i32),
             pltpu.SemaphoreType.DMA((7,)),
             pltpu.SemaphoreType.DMA((sends,)),

time: 15.1 us -> 14.6 us (0.967)
  Pallas kernels: 14.3 us -> 13.8 us
    pallas_call x1, Pallas kernels: 13.6 us -> 13.1 us  [local(): pl.pallas_call(functools.partial(kernel, devices_x, devices_y), out_shape...]
where the time goes in v3:
time: 14.6 us; the launch traced here: 14.5 us
  Pallas kernels  13.8 us (95%)
  between operations  0.66 us (5%)
    pallas_call x1, Pallas kernels, local(): pl.pallas_call(functools.partial(kernel, devices_x, devices_y), out_shape...  13.1 us
    pallas_call x1, Pallas kernels, local(): pl.pallas_call(write_out, out_shape=jax.ShapeDtypeStruct(populations.shap...  0.7 us

profile of v3, /device:TPU:0, one launch (start us, length us, event | category | flops | bytes accessed | tf_op | source)
XLA Modules:
  0.0 14.5 jit_solution(4920176729507208234)
XLA Ops:
  0.7 13.1 %lattice_step.1.source = f32[27,2,8,128]{3,2,1,0:T(8,128)S(1)} custom-call(f32[27,2,8,128]{3,2,1,0:T(8,128)} %pop_hbm.1, f32[27]{0:T(128)} %relax.1, s32[2,8,128]{2,1,0:T(8,128)} %solid_hbm.1, s32[1,1,256]{2,1,0:T(1,128)} %wall_hbm.1, s32[1,1,256]{2,1,0:T(1,128)} %normal_hbm.1, s32[1,1]{1,0:T(1,128)S(6)} %copy.10.count, s32[1,1,256]{2,1,0:T(1,128)} %ref_hbm.1, ...), custom_call_target="tpu_custom_call" | custom-call | tf_op jit(solution)/shard_map/lattice_step/pallas_call | solution.py:495
  13.8 0.7 %write_out.1 = f32[27,2,8,128]{3,2,1,0:T(8,128)} custom-call(f32[27,2,8,128]{3,2,1,0:T(8,128)S(1)} %lattice_step.1.source), custom_call_target="tpu_custom_call" | custom-call | tf_op jit(solution)/shard_map/write_out/pallas_call | solution.py:549

commit v4 on v3

--- a/solution.py
+++ b/solution.py
@@ -127,12 +127,12 @@
     stage_c,
     stage_s,
     stage_f,
+    stage_d,
     got_x,
     got_y,
     got_c,
     got_sx,
     got_sy,
-    got_sc,
     got_fx,
     got_fy,
     got_fc,
@@ -227,21 +227,11 @@
             n = tile * 3 + c
             samples[n : n + 1, :] = jnp.sum(picked[c] * factor, axis=0, keepdims=True)
     rx[1, my_y] = samples[...]
-    pl.semaphore_wait(barrier, len(greeted))
-    sample_copies = [send(samples, rx.at[1 - dx, my_y], dx, dy) for dx, dy in greeted]
 
     loads[3].wait()
     for side, y in ((0, size_y - 1), (1, 0)):
         for x in range(size_x):
             stage_s[side, x : x + 1, :] = solid[x, y : y + 1, :]
-    solid_copies = [
-        send(solid.at[size_x - 1], got_sx.at[0], 1, 0),
-        send(solid.at[0], got_sx.at[1], -1, 0),
-    ]
-    for side, dy in ((0, 1), (1, -1)):
-        solid_copies.append(send(stage_s.at[side], got_sy.at[side], 0, dy))
-        solid_copies.append(send(stage_s.at[side], got_sc.at[0, side], 1, dy))
-        solid_copies.append(send(stage_s.at[side], got_sc.at[1, side], -1, dy))
 
     coefficient = equilibrium_moments()
     for x in range(size_x):
@@ -310,6 +300,18 @@
             for x in range(size_x):
                 n = f * size_x + x
                 stage_f[side, n : n + 1, :] = fields[f, x, y : y + 1, :]
+            for way, x in ((0, size_x - 1), (1, 0)):
+                stage_d[way, side, f : f + 1, :] = fields[f, x, y : y + 1, :]
+        for way, x in ((0, size_x - 1), (1, 0)):
+            stage_d[way, side, 7:8, :] = solid[x, y : y + 1, :].astype(jnp.float32)
+    pl.semaphore_wait(barrier, len(greeted))
+    sample_copies = [send(samples, rx.at[1 - dx, my_y], dx, dy) for dx, dy in greeted]
+    solid_copies = [
+        send(solid.at[size_x - 1], got_sx.at[0], 1, 0),
+        send(solid.at[0], got_sx.at[1], -1, 0),
+    ]
+    for side, dy in ((0, 1), (1, -1)):
+        solid_copies.append(send(stage_s.at[side], got_sy.at[side], 0, dy))
     early = [
         send(post.at[18:27, size_x - 1], got_x.at[0], 1, 0),
         send(post.at[0:9, 0], got_x.at[1], -1, 0),
@@ -319,7 +321,7 @@
     for side, dy in ((0, 1), (1, -1)):
         for way, dx in ((0, 1), (1, -1)):
             early.append(send(stage_c.at[way, side], got_c.at[way, side], dx, dy))
-            early.append(send(stage_f.at[side], got_fc.at[way, side], dx, dy))
+            early.append(send(stage_d.at[way, side], got_fc.at[way, side], dx, dy))
         early.append(send(stage_y.at[side], got_y.at[side], 0, dy))
         early.append(send(stage_f.at[side], got_fy.at[side], 0, dy))
 
@@ -390,33 +392,36 @@
         edge = 0 if b > 0 else size_y - 1
         return jnp.where(line_of == edge, jnp.broadcast_to(line, value.shape), value)
 
-    for x in range(-1, size_x + 1):
+    def mark(x):
         plane = got_sx[0] if x < 0 else got_sx[1] if x == size_x else solid[x]
         for b in (-1, 0, 1):
             value = roll(plane, b, 0)
             if b != 0:
                 side = 0 if b > 0 else 1
                 if x < 0:
-                    line = got_sc[0, side, size_x - 1 : size_x, :]
+                    line = got_fc[0, side, 7:8, :].astype(jnp.int32)
                 elif x == size_x:
-                    line = got_sc[1, side, 0:1, :]
+                    line = got_fc[1, side, 7:8, :].astype(jnp.int32)
                 else:
                     line = got_sy[side, x : x + 1, :]
                 value = mend(value, line, b)
             for c in (-1, 0, 1):
                 masks[(b + 1) * 3 + c + 1, x + 1] = roll(value, c, 1)
 
+    for x in range(size_x):
+        mark(x)
+
     def gather_rows(target, index, straight, corner, f):
         for x in range(size_x):
             n = f * size_x + x
             target[index + (slice(x, x + 1),)] = straight[n : n + 1, :]
-        n = f * size_x + size_x - 1
-        target[index + (slice(size_x, size_x + 1),)] = corner[0][n : n + 1, :]
-        n = f * size_x
-        target[index + (slice(size_x + 1, size_x + 2),)] = corner[1][n : n + 1, :]
+        target[index + (slice(size_x, size_x + 1),)] = corner[0][f : f + 1, :]
+        target[index + (slice(size_x + 1, size_x + 2),)] = corner[1][f : f + 1, :]
 
     for copy in early:
         copy.wait_recv()
+    mark(-1)
+    mark(size_x)
     for side in range(2):
         for j in range(9):
             a, c = (j // 3 - 1, j % 3 - 1)
@@ -487,7 +492,7 @@
     assert size_x + 2 <= size_y == 8
     few = -(-7 * size_x // 8) * 8
     held = -(-3 * slots_all // LANES // 8) * 8
-    sends = 3 * devices_y - 1 + 8 + 16
+    sends = 3 * devices_y - 1 + 4 + 16
     vmem = pltpu.VMEM
     tile = (size_y, LANES)
     anywhere = pl.BlockSpec(memory_space=pl.ANY)
@@ -526,15 +531,15 @@
             vmem((2, 2, 8, LANES), f32),
             vmem((2, 8, LANES), i32),
             vmem((2, few, LANES), f32),
+            vmem((2, 2, 8, LANES), f32),
             vmem((2, 9) + tile, f32),
             vmem((2, lines, LANES), f32),
             vmem((2, 2, 8, LANES), f32),
             vmem((2,) + tile, i32),
             vmem((2, 8, LANES), i32),
-            vmem((2, 2, 8, LANES), i32),
             vmem((2, 7) + tile, f32),
             vmem((2, few, LANES), f32),
-            vmem((2, 2, few, LANES), f32),
+            vmem((2, 2, 8, LANES), f32),
             vmem((2, 9, 8, LANES), f32),
             vmem((2, 7, 8, LANES), f32),
             vmem((9, size_x + 2) + tile, i32),

time: 14.6 us -> 13.9 us (0.952)
  Pallas kernels: 13.8 us -> 13.1 us
    pallas_call x1, Pallas kernels: 13.1 us -> 12.4 us  [local(): pl.pallas_call(functools.partial(kernel, devices_x, devices_y), out_shape...]
where the time goes in v4:
time: 13.9 us; the launch traced here: 13.8 us
  Pallas kernels  13.1 us (94%)
  between operations  0.66 us (5%)
    pallas_call x1, Pallas kernels, local(): pl.pallas_call(functools.partial(kernel, devices_x, devices_y), out_shape...  12.4 us
    pallas_call x1, Pallas kernels, local(): pl.pallas_call(write_out, out_shape=jax.ShapeDtypeStruct(populations.shap...  0.7 us

profile of v4, /device:TPU:0, one launch (start us, length us, event | category | flops | bytes accessed | tf_op | source)
XLA Modules:
  0.0 13.8 jit_solution(6039932133528477147)
XLA Ops:
  0.7 12.4 %lattice_step.1.source = f32[27,2,8,128]{3,2,1,0:T(8,128)S(1)} custom-call(f32[27,2,8,128]{3,2,1,0:T(8,128)} %pop_hbm.1, f32[27]{0:T(128)} %relax.1, s32[2,8,128]{2,1,0:T(8,128)} %solid_hbm.1, s32[1,1,256]{2,1,0:T(1,128)} %wall_hbm.1, s32[1,1,256]{2,1,0:T(1,128)} %normal_hbm.1, s32[1,1]{1,0:T(1,128)S(6)} %copy.10.count, s32[1,1,256]{2,1,0:T(1,128)} %ref_hbm.1, ...), custom_call_target="tpu_custom_call" | custom-call | tf_op jit(solution)/shard_map/lattice_step/pallas_call | solution.py:500
  13.1 0.7 %write_out.1 = f32[27,2,8,128]{3,2,1,0:T(8,128)} custom-call(f32[27,2,8,128]{3,2,1,0:T(8,128)S(1)} %lattice_step.1.source), custom_call_target="tpu_custom_call" | custom-call | tf_op jit(solution)/shard_map/write_out/pallas_call | solution.py:554
